TPU v7x, 32 devices: a whole 2x2x4 slice. The times are simulated.
32 devices in a mesh: grp: 4 (over y, x), sub: 8 (over z, core).
Axes of the slice: x: 2, y: 2, z: 4, core: 2. Of those that a mesh axis runs over, the one named last changes fastest.
Arguments:
- bem_tiles: float32 [4096, 4096], P('grp', 'sub'), may hold values from -0.0625 to 0.0625
- leaf_inverse: float32 [4, 16, 1024, 1024], P('grp', 'sub'), may hold values from -1.5 to 1.5
- coupling: float32 [4, 16, 1024, 512], P('grp', 'sub'), may hold values from -0.0625 to 0.0625
- schur_inverse: float32 [4, 512, 512], P('grp', None, 'sub'), may hold values from -1.5 to 1.5
- leaf_load: float32 [4, 16, 1024, 128], P('grp', 'sub'), may hold values from -6 to 6
- sep_load: float32 [4, 512, 128], P('grp'), may hold values from -6 to 6
- surf_load: float32 [4096, 128], P(('grp', 'sub')), may hold values from -6 to 6
- surf_start: float32 [4096, 128], P(('grp', 'sub')), may hold values from -6 to 6
- flux_weight: float32 [4, 16, 8, 128], P('grp', 'sub'), may hold values from 0.25 to 1
- trace_weight: float32 [4, 16, 8, 128], P('grp', 'sub'), may hold values from 0.25 to 1
- leaf_sizes: int32 [4, 16], P('grp', 'sub'), may hold values from 512 to 1024
- block_counts: int32 [4, 16], P('grp', 'sub'), may hold values from 4 to 8
- block_owner: int32 [4, 16, 8, 1], P('grp', 'sub'), may hold values from 0 to 7; in each aligned block of 16 rows (0 to 15, 16 to 31, ..., all dimensions but the last counted through in order) at most 2 rows name the same one
Outputs:
- solution: float32 [4, 16, 1024, 128], P('grp', 'sub')
- sep_value: float32 [4, 512, 128], P('grp', 'sub')
- pressure: float32 [4096, 128], P(('grp', 'sub'))
Inputs may be any that keep to these rules, and one draw needn't show every extreme that they name: `block_owner`: of the 16 entries of one device, live or not, at most 2 name the same owner, and some device has 2 entries naming one owner.
All inputs are finite; a program needn't handle non-finite values.
Results may differ from a plain program's by a relative error of at most 0.00018.
Values sent between devices are 32-bit elements; how exact they have to be, the bound alone decides.
A program may use at most 128 MiB of HBM per device.

v0:
```python
import jax
import jax.numpy as jnp
from jax import lax
from jax.sharding import PartitionSpec as P

CAP = 2
SWEEPS = 3


def on_device(
    bem_tiles,
    leaf_inverse,
    coupling,
    schur_inverse,
    leaf_load,
    sep_load,
    surf_load,
    surf_start,
    flux_weight,
    trace_weight,
    leaf_sizes,
    block_counts,
    block_owner,
):
    highest = lax.Precision.HIGHEST
    parts = lax.axis_size("sub")
    here = lax.axis_index("sub")
    width = surf_load.shape[0]
    loads = surf_load.shape[1]
    leaves = leaf_inverse.shape[1]
    order = leaf_inverse.shape[2]
    blocks = order // width
    entries = leaves * blocks
    separator = schur_inverse.shape[1]
    sep_share = schur_inverse.shape[2]
    row_mask = (jnp.arange(order, dtype=jnp.int32)[None, :] < leaf_sizes[0][:, None]).astype(
        jnp.float32
    )[:, :, None]
    active = (
        (jnp.arange(blocks, dtype=jnp.int32)[None, :] < block_counts[0][:, None])
        .astype(jnp.float32)
        .reshape(entries)
    )
    owner = block_owner[0, :, :, 0].reshape(entries)
    picker = (owner[:, None] == jnp.arange(parts, dtype=jnp.int32)[None, :]).astype(jnp.float32)
    live_pick = picker * active[:, None]
    flux_scale = flux_weight[0].reshape(entries, width)[:, :, None]
    trace_scale = (trace_weight[0].reshape(entries, width) * active[:, None])[:, :, None]
    position = jnp.arange(entries, dtype=jnp.int32)
    earlier = (position[:, None] > position[None, :]) & (owner[:, None] == owner[None, :])
    slot_index = jnp.sum(earlier.astype(jnp.int32), axis=1)
    target = owner * CAP + slot_index
    placing = (jnp.arange(parts * CAP, dtype=jnp.int32)[:, None] == target[None, :]).astype(
        jnp.float32
    )
    schur_full = lax.all_gather(schur_inverse[0], "sub", axis=1, tiled=True)
    pressure = surf_start
    sep_value = jnp.zeros((separator, loads), jnp.float32)
    solution = jnp.zeros((leaves, order, loads), jnp.float32)
    for sweep in range(SWEEPS):
        column = lax.all_gather(pressure, "grp", axis=0, tiled=True)

        def tile_product(start, count, column=column):
            return jnp.dot(bem_tiles, column, precision=highest, preferred_element_type=jnp.float32)

        applied = lax.psum_scatter(
            tile_product(jnp.int32(0), lax.axis_size("sub") * width),
            "sub",
            scatter_dimension=0,
            tiled=True,
        )
        surface_patch = lax.all_gather(pressure, "sub", axis=0, tiled=True).reshape(
            parts, width, loads
        )
        flux = jnp.einsum("eo,oil->eil", live_pick, surface_patch, precision=highest) * flux_scale
        flux = flux.reshape(leaves, order, loads)
        pulled = jnp.einsum("jrs,sl->jrl", coupling[0], sep_value, precision=highest)
        rhs = (leaf_load[0] - pulled - flux) * row_mask
        solution = jnp.einsum("jrc,jcl->jrl", leaf_inverse[0], rhs, precision=highest) * row_mask
        partial_sum = jnp.einsum("jrs,jrl->sl", coupling[0], solution, precision=highest)
        summed = lax.psum(partial_sum, "sub")
        sep_value = jnp.dot(
            schur_full, sep_load[0] - summed, precision=highest, preferred_element_type=jnp.float32
        )
        weighted = solution.reshape(entries, width, loads) * trace_scale
        outgoing = jnp.dot(
            placing,
            weighted.reshape(entries, width * loads),
            precision=highest,
            preferred_element_type=jnp.float32,
        )
        incoming = lax.all_to_all(
            outgoing.reshape(parts, CAP, width, loads),
            "sub",
            split_axis=0,
            concat_axis=0,
            tiled=True,
        )
        trace = jnp.sum(incoming, axis=(0, 1))
        pressure = surf_load + applied + trace
    sep_rows_out = lax.dynamic_slice_in_dim(sep_value, here * sep_share, sep_share, 0)
    return (solution[None], sep_rows_out[None], pressure)


def solution(mesh):
    return jax.shard_map(
        on_device,
        mesh=mesh,
        in_specs=(
            P("grp", "sub"),
            P("grp", "sub", None, None),
            P("grp", "sub", None, None),
            P("grp", None, "sub"),
            P("grp", "sub", None, None),
            P("grp", None, None),
            P(("grp", "sub"), None),
            P(("grp", "sub"), None),
            P("grp", "sub", None, None),
            P("grp", "sub", None, None),
            P("grp", "sub"),
            P("grp", "sub"),
            P("grp", "sub", None, None),
        ),
        out_specs=(P("grp", "sub", None, None), P("grp", "sub", None), P(("grp", "sub"), None)),
        check_vma=False,
    )
```

profile of v0, /device:TPU:0, one launch (start us, length us, event | category | flops | bytes accessed | tf_op | source)
XLA Modules:
  0.0 464.7 jit_solution(11380869395240890339)
XLA Ops:
  7.3 10.9 %all_gather.23 = f32[512,128]{1,0:T(8,128)S(1)} all-gather(f32[128,128]{1,0:T(8,128)} %param.20), channel_id=1, replica_groups=mesh['grp'=4,'sub'=8] {'grp'}, dimensions={0}, use_global_device_ids=true | all-gather | bytes 327680 | tf_op jit(solution)/shard_map/all_gather | solution.py:61
  18.2 2.6 fusion.127
  20.8 15.6 %all_gather.21 = f32[1024,128]{1,0:T(8,128)S(1)} all-gather(f32[128,128]{1,0:T(8,128)} %param.20), channel_id=1, replica_groups=mesh['grp'=4,'sub'=8] {'sub'}, dimensions={0}, use_global_device_ids=true | all-gather | bytes 589824 | tf_op jit(solution)/shard_map/all_gather | solution.py:72
  39.7 1.3 copy.80
  41.0 1.6 copy.75
  42.6 7.2 %fusion.51 = f32[2,1024,128]{1,2,0:T(8,128)S(1)} fusion(f32[2,1024,128]{1,2,0:T(8,128)} %copy.80, f32[1,2,1024,512]{3,2,1,0:T(8,128)} %param.15, f32[1,2,1024,128]{2,3,1,0:T(8,128)S(1)} %copy.75, f32[2,1024]{1,0:T(2,128)S(1)} %compare_convert_fusion), kind=kOutput, calls=%fused_computation.29 | convolution fusion | flops 1611399168 | bytes 7348224 | tf_op jit(solution)/shard_map/jrs,sl->jrl/dot_general | solution.py:77
  49.8 12.1 %fusion.57 = f32[2,1024,128]{1,2,0:T(8,128)} fusion(f32[2,1024,128]{1,2,0:T(8,128)S(1)} %fusion.51, f32[1,2,1024,1024]{3,2,1,0:T(8,128)} %param.14, f32[2,1024]{1,0:T(2,128)S(1)} %compare_convert_fusion), kind=kOutput, calls=%fused_computation.34 | convolution fusion | flops 3221487616 | bytes 10493952 | tf_op jit(solution)/shard_map/jrc,jcl->jrl/dot_general | solution.py:79
  62.0 1.6 copy.81
  65.0 2.4 fusion.85
  68.7 5.2 %all-to-all-start = ((f32[8,2,128,128]{3,2,1,0:T(8,128)}), f32[8,2,128,128]{3,2,1,0:T(8,128)}, u32[]{:S(2)}, u32[]{:S(2)}) async-start(f32[8,2,128,128]{3,2,1,0:T(8,128)} %copy.83), calls=%async_computation.1 | async-start | bytes 2097152 | tf_op jit(solution)/shard_map/all_to_all | solution.py:92
  74.3 5.7 %fusion.69 = f32[512,128]{0,1:T(8,128)} fusion(f32[2,1024,128]{1,2,0:T(8,128)} %fusion.57, f32[1,2,1024,512]{3,2,1,0:T(8,128)} %param.15), kind=kOutput, calls=%fused_computation.40 | convolution fusion | flops 1610612736 | bytes 5505024 | tf_op jit(solution)/shard_map/jrs,jrl->sl/dot_general | solution.py:80
  81.8 20.1 %all-to-all-done = f32[8,2,128,128]{3,2,1,0:T(8,128)} async-done(((f32[8,2,128,128]{3,2,1,0:T(8,128)}), f32[8,2,128,128]{3,2,1,0:T(8,128)}, u32[]{:S(2)}, u32[]{:S(2)}) %all-to-all-start) | async-done | bytes 1048608 | tf_op jit(solution)/shard_map/all_to_all | solution.py:92
  101.9 1.9 reduce_sum.37
  104.8 14.8 %all_gather.24 = f32[1024,128]{1,0:T(8,128)S(1)} all-gather(f32[128,128]{1,0:T(8,128)S(1)} %add_add_fusion.2), channel_id=1, replica_groups=mesh['grp'=4,'sub'=8] {'sub'}, dimensions={0}, use_global_device_ids=true | all-gather | bytes 589824 | tf_op jit(solution)/shard_map/all_gather | solution.py:72
  119.5 1.8 convolution_multiply_fusion.1
  122.7 2.6 copy.86
  125.2 15.9 %all-reduce.4.cloned.1.call-done = f32[512,128]{0,1:T(8,128)} async-done(((f32[512,128]{0,1:T(8,128)}), f32[512,128]{0,1:T(8,128)}) %all-reduce.4.cloned.1.call-update) | async-done | bytes 262160 | tf_op jit(solution)/shard_map/psum | solution.py:81
  141.2 22.9 %all-gather.3.cloned.1.call-done = f32[1,512,512]{1,2,0:T(8,128)} async-done(((f32[1,512,64]{1,2,0:T(8,128)}), f32[1,512,512]{1,2,0:T(8,128)}) %all-gather.3.cloned.1.call-update) | async-done | bytes 1048592 | tf_op jit(solution)/shard_map/all_gather | solution.py:56
  164.1 2.0 convolution_bitcast_fusion.3
  166.1 7.2 %fusion.42 = f32[2,1024,128]{1,2,0:T(8,128)S(1)} fusion(f32[2,1024,128]{1,2,0:T(8,128)} %copy.86, f32[128,512,1]{1,0,2:T(8,128)S(1)} %convolution_bitcast_fusion.3, f32[1,2,1024,512]{3,2,1,0:T(8,128)} %param.15, f32[1,2,1024,128]{2,3,1,0:T(8,128)} %copy-done.2, f32[2,1024]{1,0:T(2,128)S(1)} %compare_convert_fusion), kind=kOutput, calls=%fused_computation.26 | convolution fusion | flops 1611399168 | bytes 7610368 | tf_op jit(solution)/shard_map/jrs,sl->jrl/dot_general | solution.py:77
  173.3 12.1 %fusion.63 = f32[2,1024,128]{1,2,0:T(8,128)} fusion(f32[2,1024,128]{1,2,0:T(8,128)S(1)} %fusion.42, f32[1,2,1024,1024]{3,2,1,0:T(8,128)} %param.14, f32[2,1024]{1,0:T(2,128)S(1)} %compare_convert_fusion), kind=kOutput, calls=%fused_computation.36 | convolution fusion | flops 3221487616 | bytes 10493952 | tf_op jit(solution)/shard_map/jrc,jcl->jrl/dot_general | solution.py:79
  185.4 2.6 copy.88
  188.0 2.4 reshape.166
  190.4 2.5 fusion.83
  194.0 4.2 all-to-all-start.1
  198.5 5.7 %fusion.72 = f32[512,128]{0,1:T(8,128)} fusion(f32[2,1024,128]{1,2,0:T(8,128)} %fusion.63, f32[1,2,1024,512]{3,2,1,0:T(8,128)} %param.15), kind=kOutput, calls=%fused_computation.41 | convolution fusion | flops 1610612736 | bytes 5505024 | tf_op jit(solution)/shard_map/jrs,jrl->sl/dot_general | solution.py:80
  204.2 9.0 %all_gather.25 = f32[512,128]{1,0:T(8,128)S(1)} all-gather(f32[128,128]{1,0:T(8,128)S(1)} %add_add_fusion.2), channel_id=1, replica_groups=mesh['grp'=4,'sub'=8] {'grp'}, dimensions={0}, use_global_device_ids=true | all-gather | bytes 327680 | tf_op jit(solution)/shard_map/all_gather | solution.py:61
  213.2 3.1 convolution_bitcast_fusion.1
  216.3 1.6 copy.87
  217.9 48.1 %all-reduce.6.cloned.1.call-done = f32[512,128]{0,1:T(8,128)} async-done(((f32[512,128]{0,1:T(8,128)}), f32[512,128]{0,1:T(8,128)}) %all-reduce.6.cloned.1.call-update) | async-done | bytes 262160 | tf_op jit(solution)/shard_map/psum | solution.py:81
  266.0 2.7 convolution_bitcast_fusion.2
  270.8 28.2 %reduce-scatter.6.cloned.1.call-done = f32[128,128]{0,1:T(8,128)} async-done(((f32[1024,128]{0,1:T(8,128)}), f32[128,128]{0,1:T(8,128)}) %reduce-scatter.6.cloned.1.call-update) | async-done | bytes 65552 | tf_op jit(solution)/shard_map/reduce_scatter | solution.py:66
  299.9 14.9 %all_gather.26 = f32[1024,128]{0,1:T(8,128)S(1)} all-gather(f32[128,128]{0,1:T(8,128)S(1)} %add_add_fusion.1), channel_id=1, replica_groups=mesh['grp'=4,'sub'=8] {'sub'}, dimensions={0}, use_global_device_ids=true | all-gather | bytes 589824 | tf_op jit(solution)/shard_map/all_gather | solution.py:72
  315.7 2.0 copy.93
  317.8 2.1 convolution_multiply_fusion
  321.1 2.6 copy.95
  323.7 7.2 %fusion.33 = f32[2,1024,128]{1,2,0:T(8,128)S(1)} fusion(f32[2,1024,128]{1,2,0:T(8,128)} %copy.95, f32[128,512,1]{1,0,2:T(8,128)} %convolution_bitcast_fusion.2, f32[1,2,1024,512]{3,2,1,0:T(8,128)} %param.15, f32[1,2,1024,128]{2,3,1,0:T(8,128)} %copy-done.2, f32[2,1024]{1,0:T(2,128)S(1)} %compare_convert_fusion), kind=kOutput, calls=%fused_computation.23 | convolution fusion | flops 1611399168 | bytes 7610368 | tf_op jit(solution)/shard_map/jrs,sl->jrl/dot_general | solution.py:77
  330.9 12.1 %fusion.66 = f32[2,128,1024]{2,1,0:T(8,128)} fusion(f32[2,1024,128]{1,2,0:T(8,128)S(1)} %fusion.33, f32[1,2,1024,1024]{3,2,1,0:T(8,128)} %param.14, f32[2,1024]{1,0:T(2,128)S(1)} %compare_convert_fusion), kind=kOutput, calls=%fused_computation.37 | convolution fusion | flops 3221487616 | bytes 10493952 | tf_op jit(solution)/shard_map/jrc,jcl->jrl/dot_general | solution.py:79
  343.0 2.6 copy.97
  345.7 2.4 reshape.169
  348.1 2.4 fusion.81
  351.7 4.2 all-to-all-start.2
  356.2 5.3 %fusion.75 = f32[512,128]{0,1:T(8,128)} fusion(f32[1,2,1024,512]{3,2,1,0:T(8,128)} %param.15, f32[2,128,1024]{2,1,0:T(8,128)S(1)} %copy-done.1), kind=kOutput, calls=%fused_computation.42 | convolution fusion | flops 1610612736 | bytes 5505024 | tf_op jit(solution)/shard_map/jrs,jrl->sl/dot_general | solution.py:80
  361.6 10.3 %all_gather.27 = f32[512,128]{0,1:T(8,128)S(1)} all-gather(f32[128,128]{0,1:T(8,128)S(1)} %add_add_fusion.1), channel_id=1, replica_groups=mesh['grp'=4,'sub'=8] {'grp'}, dimensions={0}, use_global_device_ids=true | all-gather | bytes 327680 | tf_op jit(solution)/shard_map/all_gather | solution.py:61
  371.9 3.1 convolution_bitcast_fusion
  376.3 47.2 %all-reduce.8.cloned.1.call-done = f32[512,128]{0,1:T(8,128)} async-done(((f32[512,128]{0,1:T(8,128)}), f32[512,128]{0,1:T(8,128)}) %all-reduce.8.cloned.1.call-update) | async-done | bytes 262160 | tf_op jit(solution)/shard_map/psum | solution.py:81
  423.6 3.1 fusion.87
  428.7 27.4 %reduce-scatter.8.cloned.1.call-done = f32[128,128]{0,1:T(8,128)} async-done(((f32[1024,128]{0,1:T(8,128)}), f32[128,128]{0,1:T(8,128)}) %reduce-scatter.8.cloned.1.call-update) | async-done | bytes 65552 | tf_op jit(solution)/shard_map/reduce_scatter | solution.py:66
  (73 shorter events, 23.6 us)
Async XLA Ops:
  7.2 11.0 %copy-start = (f32[1024,512]{1,0:T(8,128)S(1)}, f32[1024,512]{1,0:T(8,128)}, u32[]{:S(2)}) copy-start(f32[1024,512]{1,0:T(8,128)} %param.13) | copy-start | bytes 6291460
  7.2 29.7 %copy-start.9 = (s32[1,2,8,1]{2,3,1,0:T(1,128)S(1)}, s32[1,2,8,1]{2,3,1,0:T(1,128)}, u32[]{:S(2)}) copy-start(s32[1,2,8,1]{2,3,1,0:T(1,128)} %param.25) | copy-start | bytes 196
  7.2 30.6 %copy-start.11 = (s32[1,2]{1,0:T(1,128)S(1)}, s32[1,2]{1,0:T(1,128)}, u32[]{:S(2)}) copy-start(s32[1,2]{1,0:T(1,128)} %param.24) | copy-start | bytes 28
  7.2 30.8 %copy-start.10 = (s32[1,2]{1,0:T(1,128)S(1)}, s32[1,2]{1,0:T(1,128)}, u32[]{:S(2)}) copy-start(s32[1,2]{1,0:T(1,128)} %param.23) | copy-start | bytes 28
  7.2 30.8 %copy-start.4 = (f32[1,2,8,128]{3,2,1,0:T(8,128)S(1)}, f32[1,2,8,128]{3,2,1,0:T(8,128)}, u32[]{:S(2)}) copy-start(f32[1,2,8,128]{3,2,1,0:T(8,128)} %param.21) | copy-start | bytes 24580
  7.2 30.9 %copy-start.5 = (f32[1,2,8,128]{3,2,1,0:T(8,128)S(1)}, f32[1,2,8,128]{3,2,1,0:T(8,128)}, u32[]{:S(2)}) copy-start(f32[1,2,8,128]{3,2,1,0:T(8,128)} %param.22) | copy-start | bytes 24580
  7.2 96.6 %reduce-scatter.4.cloned.1.call-start = ((), (), s32[]{:S(2)}) async-start(), calls=%async_computation.7 | async-start | bytes 589824 | tf_op jit(solution)/shard_map/reduce_scatter | solution.py:66
  37.6 24.3 %copy-start.6 = (s32[16]{0:T(128)}, s32[16]{0:T(128)S(1)}, u32[]{:S(2)}) copy-start(s32[16]{0:T(128)S(1)} %eq.58) | copy-start | bytes 196
  42.6 19.3 %copy-start.2 = (f32[1,2,1024,128]{2,3,1,0:T(8,128)}, f32[1,2,1024,128]{2,3,1,0:T(8,128)S(1)}, u32[]{:S(2)}) copy-start(f32[1,2,1024,128]{2,3,1,0:T(8,128)S(1)} %copy.75) | copy-start | bytes 3145732
  61.9 5.5 %copy-start.7 = (s32[16]{0:T(128)}, s32[16]{0:T(128)S(1)}, u32[]{:S(2)}) copy-start(s32[16]{0:T(128)S(1)} %multiply_add_fusion.1) | copy-start | bytes 196
  68.7 33.3 %all-to-all-start = ((f32[8,2,128,128]{3,2,1,0:T(8,128)}), f32[8,2,128,128]{3,2,1,0:T(8,128)}, u32[]{:S(2)}, u32[]{:S(2)}) async-start(f32[8,2,128,128]{3,2,1,0:T(8,128)} %copy.83), calls=%async_computation.1 | async-start | bytes 2097152 | tf_op jit(solution)/shard_map/all_to_all | solution.py:92
  73.8 67.3 %all-reduce.4.cloned.1.call-start = ((), (), s32[]{:S(2)}) async-start(), calls=%async_computation.6 | async-start | bytes 524288 | tf_op jit(solution)/shard_map/psum | solution.py:81
  80.0 84.1 %all-gather.3.cloned.1.call-start = ((), (), s32[]{:S(2)}) async-start(), calls=%async_computation.12 | async-start | bytes 1179648 | tf_op jit(solution)/shard_map/all_gather | solution.py:56
  194.0 74.8 %all-to-all-start.1 = ((f32[8,2,128,128]{3,2,1,0:T(8,128)}), f32[8,2,128,128]{3,2,1,0:T(8,128)}, u32[]{:S(2)}, u32[]{:S(2)}) async-start(f32[8,2,128,128]{3,2,1,0:T(8,128)} %copy.90), calls=%async_computation.3 | async-start | bytes 2097152 | tf_op jit(solution)/shard_map/all_to_all | solution.py:92
  198.3 67.8 %all-reduce.6.cloned.1.call-start = ((), (), s32[]{:S(2)}) async-start(), calls=%async_computation.8 | async-start | bytes 524288 | tf_op jit(solution)/shard_map/psum | solution.py:81
  204.2 94.8 %reduce-scatter.6.cloned.1.call-start = ((), (), s32[]{:S(2)}) async-start(), calls=%async_computation.9 | async-start | bytes 589824 | tf_op jit(solution)/shard_map/reduce_scatter | solution.py:66
  343.0 5.0 %copy-start.8 = (s32[16]{0:T(128)S(1)}, s32[16]{0:T(128)}, u32[]{:S(2)}) copy-start(s32[16]{0:T(128)} %copy-done.7) | copy-start | bytes 196
  350.5 5.7 %copy-start.1 = (f32[2,128,1024]{2,1,0:T(8,128)S(1)}, f32[2,128,1024]{2,1,0:T(8,128)}, u32[]{:S(2)}) copy-start(f32[2,128,1024]{2,1,0:T(8,128)} %fusion.66) | copy-start | bytes 3145732
  351.7 75.6 %all-to-all-start.2 = ((f32[8,2,128,128]{3,2,1,0:T(8,128)}), f32[8,2,128,128]{3,2,1,0:T(8,128)}, u32[]{:S(2)}, u32[]{:S(2)}) async-start(f32[8,2,128,128]{3,2,1,0:T(8,128)} %copy.99), calls=%async_computation.5 | async-start | bytes 2097152 | tf_op jit(solution)/shard_map/all_to_all | solution.py:92
  356.0 67.6 %all-reduce.8.cloned.1.call-start = ((), (), s32[]{:S(2)}) async-start(), calls=%async_computation.10 | async-start | bytes 524288 | tf_op jit(solution)/shard_map/psum | solution.py:81
  361.6 94.5 %reduce-scatter.8.cloned.1.call-start = ((), (), s32[]{:S(2)}) async-start(), calls=%async_computation.11 | async-start | bytes 589824 | tf_op jit(solution)/shard_map/reduce_scatter | solution.py:66
  371.9 84.2 %copy-start.3 = (f32[128,128]{0,1:T(8,128)S(1)}, f32[128,128]{0,1:T(8,128)}, u32[]{:S(2)}) copy-start(f32[128,128]{0,1:T(8,128)} %copy.87) | copy-start | bytes 196612
Sparse Core Ops, SparseCore 0:
  20.9 31.6 reduce-scatter.3
  80.1 61.0 all-reduce.3
  142.8 21.2 all-gather.2
  204.3 61.7 all-reduce.5
  268.7 30.1 reduce-scatter.5
  361.7 61.8 all-reduce.7
  425.8 30.1 reduce-scatter.7
where the time goes:
time: 468 us; the launch traced here: 465 us
  waiting for transfers between devices  211 us (45%)
  matrix products  104 us (22%)
  blocking collectives  75.4 us (16%)
  local copies, waits for them, and re-layouts  37.4 us (8%)
  starting transfers between devices  14.7 us (3%)
  between operations  14.6 us (3%)
  other arithmetic  8.24 us (2%)
    psum x3, waiting for transfers between devices, on_device(): summed = lax.psum(partial_sum, 'sub')  111 us
    reduce_scatter x3, waiting for transfers between devices, on_device(): lax.psum_scatter(tile_product(jnp.int32(0), lax.axis_size('sub') * width)...  55.5 us
    all_gather x3, blocking collectives, on_device(): lax.all_gather(pressure, 'sub', axis=0, tiled=True)  45.3 us
    dot_general x3, matrix products, on_device(): jnp.einsum('jrc,jcl->jrl', leaf_inverse[0], rhs, precision=highest)  36.3 us
    all_gather x3, blocking collectives, on_device(): column = lax.all_gather(pressure, 'grp', axis=0, tiled=True)  30.1 us
    all_gather x1, waiting for transfers between devices, on_device(): schur_full = lax.all_gather(schur_inverse[0], 'sub', axis=1, tiled=True)  22.9 us
    dot_general x3, matrix products, on_device(): jnp.einsum('jrs,sl->jrl', coupling[0], sep_value, precision=highest)  21.6 us
    all_to_all x3, waiting for transfers between devices, on_device(): lax.all_to_all(outgoing.reshape(parts, CAP, width, loads), 'sub', split_a...  20.1 us
  transfers between devices with their start and end apart: 10, of which 7 were waited for; matrix products, arithmetic and copies ran while one was open for 17% of the time, Pallas kernels for 0%

commit v1 on v0

--- a/solution.py
+++ b/solution.py
@@ -78,7 +78,11 @@
         rhs = (leaf_load[0] - pulled - flux) * row_mask
         solution = jnp.einsum("jrc,jcl->jrl", leaf_inverse[0], rhs, precision=highest) * row_mask
         partial_sum = jnp.einsum("jrs,jrl->sl", coupling[0], solution, precision=highest)
-        summed = lax.psum(partial_sum, "sub")
+        count_2 = lax.axis_size("sub")
+        summed, stride = (partial_sum, 1)
+        while stride < count_2:
+            summed = summed + lax.ppermute(summed, "sub", [(i, i ^ stride) for i in range(count_2)])
+            stride = 2 * stride
         sep_value = jnp.dot(
             schur_full, sep_load[0] - summed, precision=highest, preferred_element_type=jnp.float32
         )

time: 468 us -> 353 us (0.75)
  waiting for transfers between devices: 211 us -> 76.7 us
  starting transfers between devices: 14.7 us -> 26.9 us
  other arithmetic: 8.24 us -> 13.3 us
    psum x3 -> x0, waiting for transfers between devices: 111 us -> none  [on_device(): summed = lax.psum(partial_sum, 'sub')]
    ppermute x0 -> x9, waiting for transfers between devices: none -> 76.3 us  [on_device(): lax.ppermute(summed, 'sub', [(i, i ^ stride) for i in range(count_2)])]
    reduce_scatter x3, waiting for transfers between devices: 55.5 us -> 0.02 us  [on_device(): lax.psum_scatter(tile_product(jnp.int32(0), lax.axis_size('sub') * width)...]
    all_gather x1, waiting for transfers between devices: 22.9 us -> 0.01 us  [on_device(): schur_full = lax.all_gather(schur_inverse[0], 'sub', axis=1, tiled=True)]
    all_to_all x3, waiting for transfers between devices: 20.1 us -> 0.01 us  [on_device(): lax.all_to_all(outgoing.reshape(parts, CAP, width, loads), 'sub', split_a...]
    ppermute x0 -> x9, starting transfers between devices: none -> 12.3 us  [on_device(): lax.ppermute(summed, 'sub', [(i, i ^ stride) for i in range(count_2)])]
    add x0 -> x6, other arithmetic: none -> 5.1 us  [on_device(): summed + lax.ppermute(summed, 'sub', [(i, i ^ stride) for i in range(coun...]
  transfers between devices with their start and end apart: 10 -> 16, of which waited for: 7 -> 7; matrix products, arithmetic and copies ran while one was open for 17% -> 23% of each run, Pallas kernels for 0% -> 0%
where the time goes in v1:
time: 353 us; the launch traced here: 349 us
  matrix products  102 us (29%)
  blocking collectives  78.9 us (22%)
  waiting for transfers between devices  76.7 us (22%)
  local copies, waits for them, and re-layouts  36.4 us (10%)
  starting transfers between devices  26.9 us (8%)
  between operations  14.3 us (4%)
  other arithmetic  13.3 us (4%)
    ppermute x9, waiting for transfers between devices, on_device(): lax.ppermute(summed, 'sub', [(i, i ^ stride) for i in range(count_2)])  76.3 us
    all_gather x3, blocking collectives, on_device(): lax.all_gather(pressure, 'sub', axis=0, tiled=True)  49.1 us
    dot_general x3, matrix products, on_device(): jnp.einsum('jrc,jcl->jrl', leaf_inverse[0], rhs, precision=highest)  36.3 us
    all_gather x3, blocking collectives, on_device(): column = lax.all_gather(pressure, 'grp', axis=0, tiled=True)  29.8 us
    dot_general x3, matrix products, on_device(): jnp.einsum('jrs,sl->jrl', coupling[0], sep_value, precision=highest)  21.5 us
    dot_general x3, matrix products, on_device(): jnp.einsum('jrs,jrl->sl', coupling[0], solution, precision=highest)  15.3 us
    all_to_all x3, starting transfers between devices, on_device(): lax.all_to_all(outgoing.reshape(parts, CAP, width, loads), 'sub', split_a...  13.8 us
    ppermute x9, starting transfers between devices, on_device(): lax.ppermute(summed, 'sub', [(i, i ^ stride) for i in range(count_2)])  12.3 us
  transfers between devices with their start and end apart: 16, of which 7 were waited for; matrix products, arithmetic and copies ran while one was open for 23% of the time, Pallas kernels for 0%

profile of v1, /device:TPU:0, one launch (start us, length us, event | category | flops | bytes accessed | tf_op | source)
XLA Modules:
  0.0 348.9 jit_solution(17141770843342330073)
XLA Ops:
  7.3 10.9 %all_gather.23 = f32[512,128]{1,0:T(8,128)S(1)} all-gather(f32[128,128]{1,0:T(8,128)} %param.20), channel_id=1, replica_groups=mesh['grp'=4,'sub'=8] {'grp'}, dimensions={0}, use_global_device_ids=true | all-gather | bytes 327680 | tf_op jit(solution)/shard_map/all_gather | solution.py:61
  18.1 2.6 fusion.130
  20.8 15.6 %all_gather.21 = f32[1024,128]{1,0:T(8,128)S(1)} all-gather(f32[128,128]{1,0:T(8,128)} %param.20), channel_id=1, replica_groups=mesh['grp'=4,'sub'=8] {'sub'}, dimensions={0}, use_global_device_ids=true | all-gather | bytes 589824 | tf_op jit(solution)/shard_map/all_gather | solution.py:72
  41.0 1.6 copy.77
  42.6 7.1 %fusion.51 = f32[2,1024,128]{1,2,0:T(8,128)S(1)} fusion(f32[2,1024,128]{1,2,0:T(8,128)} %copy.82, f32[1,2,1024,512]{3,2,1,0:T(8,128)} %param.15, f32[1,2,1024,128]{2,3,1,0:T(8,128)S(1)} %copy.77, f32[2,1024]{1,0:T(2,128)S(1)} %compare_convert_fusion), kind=kOutput, calls=%fused_computation.29 | convolution fusion | flops 1611399168 | bytes 7348224 | tf_op jit(solution)/shard_map/jrs,sl->jrl/dot_general | solution.py:77
  49.8 12.1 %fusion.57 = f32[2,1024,128]{1,2,0:T(8,128)} fusion(f32[2,1024,128]{1,2,0:T(8,128)S(1)} %fusion.51, f32[1,2,1024,1024]{3,2,1,0:T(8,128)} %param.14, f32[2,1024]{1,0:T(2,128)S(1)} %compare_convert_fusion), kind=kOutput, calls=%fused_computation.34 | convolution fusion | flops 3221487616 | bytes 10493952 | tf_op jit(solution)/shard_map/jrc,jcl->jrl/dot_general | solution.py:79
  64.9 2.4 fusion.85
  68.6 5.4 %all-to-all-start = ((f32[8,2,128,128]{3,2,1,0:T(8,128)}), f32[8,2,128,128]{3,2,1,0:T(8,128)}, u32[]{:S(2)}, u32[]{:S(2)}) async-start(f32[8,2,128,128]{3,2,1,0:T(8,128)} %copy.85), calls=%async_computation.1 | async-start | bytes 2097152 | tf_op jit(solution)/shard_map/all_to_all | solution.py:96
  74.7 4.9 %fusion.69 = f32[512,128]{0,1:T(8,128)S(1)} fusion(f32[2,1024,128]{1,2,0:T(8,128)} %fusion.57, f32[1,2,1024,512]{3,2,1,0:T(8,128)} %param.15), kind=kOutput, calls=%fused_computation.40 | convolution fusion | flops 1610612736 | bytes 5505024 | tf_op jit(solution)/shard_map/jrs,jrl->sl/dot_general | solution.py:80
  82.1 1.9 collective-permute-start.1
  85.1 20.8 %collective-permute-done.1 = f32[512,128]{0,1:T(8,128)} collective-permute-done((f32[512,128]{0,1:T(8,128)}, f32[512,128]{0,1:T(8,128)}, u32[]{:S(2)}, u32[]{:S(2)}) %collective-permute-start.1) | collective-permute-done | bytes 262176 | tf_op jit(solution)/shard_map/ppermute | solution.py:84
  105.9 1.8 add.68
  107.7 4.6 %collective-permute-start.2 = (f32[512,128]{0,1:T(8,128)}, f32[512,128]{0,1:T(8,128)}, u32[]{:S(2)}, u32[]{:S(2)}) collective-permute-start(f32[512,128]{0,1:T(8,128)} %add.68), channel_id=1, source_target_pairs={{0,4},{1,5},{2,6},{3,7},{4,0},{5,1},{6,2},{7,3},{8,12},{9,13},{10,... | collective-permute-start | bytes 786440 | tf_op jit(solution)/shard_map/ppermute | solution.py:84
  112.3 1.9 reduce_sum.37
  115.2 18.9 %all_gather.24 = f32[1024,128]{1,0:T(8,128)S(1)} all-gather(f32[128,128]{1,0:T(8,128)S(1)} %add_add_fusion.2), channel_id=1, replica_groups=mesh['grp'=4,'sub'=8] {'sub'}, dimensions={0}, use_global_device_ids=true | all-gather | bytes 589824 | tf_op jit(solution)/shard_map/all_gather | solution.py:72
  134.1 1.8 convolution_multiply_fusion.1
  137.1 2.5 copy.88
  139.7 2.1 convolution_bitcast_fusion.3
  141.8 7.2 %fusion.42 = f32[2,1024,128]{1,2,0:T(8,128)S(1)} fusion(f32[2,1024,128]{1,2,0:T(8,128)} %copy.88, f32[128,512,1]{1,0,2:T(8,128)S(1)} %convolution_bitcast_fusion.3, f32[1,2,1024,512]{3,2,1,0:T(8,128)} %param.15, f32[1,2,1024,128]{2,3,1,0:T(8,128)} %copy-done.2, f32[2,1024]{1,0:T(2,128)S(1)} %compare_convert_fusion), kind=kOutput, calls=%fused_computation.26 | convolution fusion | flops 1611399168 | bytes 7610368 | tf_op jit(solution)/shard_map/jrs,sl->jrl/dot_general | solution.py:77
  149.0 12.1 %fusion.63 = f32[2,1024,128]{1,2,0:T(8,128)} fusion(f32[2,1024,128]{1,2,0:T(8,128)S(1)} %fusion.42, f32[1,2,1024,1024]{3,2,1,0:T(8,128)} %param.14, f32[2,1024]{1,0:T(2,128)S(1)} %compare_convert_fusion), kind=kOutput, calls=%fused_computation.36 | convolution fusion | flops 3221487616 | bytes 10493952 | tf_op jit(solution)/shard_map/jrc,jcl->jrl/dot_general | solution.py:79
  161.1 2.5 copy.90
  163.6 2.4 reshape.166
  166.0 2.5 fusion.83
  169.7 4.2 %all-to-all-start.1 = ((f32[8,2,128,128]{3,2,1,0:T(8,128)}), f32[8,2,128,128]{3,2,1,0:T(8,128)}, u32[]{:S(2)}, u32[]{:S(2)}) async-start(f32[8,2,128,128]{3,2,1,0:T(8,128)} %copy.92), calls=%async_computation.3 | async-start | bytes 2097152 | tf_op jit(solution)/shard_map/all_to_all | solution.py:96
  174.0 8.3 %all_gather.25 = f32[512,128]{1,0:T(8,128)S(1)} all-gather(f32[128,128]{1,0:T(8,128)S(1)} %add_add_fusion.2), channel_id=1, replica_groups=mesh['grp'=4,'sub'=8] {'grp'}, dimensions={0}, use_global_device_ids=true | all-gather | bytes 327680 | tf_op jit(solution)/shard_map/all_gather | solution.py:61
  182.2 3.1 convolution_bitcast_fusion.1
  185.4 5.0 %fusion.72 = f32[512,128]{0,1:T(8,128)S(1)} fusion(f32[2,1024,128]{1,2,0:T(8,128)} %fusion.63, f32[1,2,1024,512]{3,2,1,0:T(8,128)} %param.15), kind=kOutput, calls=%fused_computation.41 | convolution fusion | flops 1610612736 | bytes 5505024 | tf_op jit(solution)/shard_map/jrs,jrl->sl/dot_general | solution.py:80
  192.0 1.9 collective-permute-start.4
  194.0 13.0 %collective-permute-done.4 = f32[512,128]{0,1:T(8,128)S(1)} collective-permute-done((f32[512,128]{0,1:T(8,128)S(1)}, f32[512,128]{0,1:T(8,128)S(1)}, u32[]{:S(2)}, u32[]{:S(2)}) %collective-permute-start.4) | collective-permute-done | bytes 262176 | tf_op jit(solution)/shard_map/ppermute | solution.py:84
  209.3 13.9 %collective-permute-done.5 = f32[512,128]{0,1:T(8,128)} collective-permute-done((f32[512,128]{0,1:T(8,128)}, f32[512,128]{0,1:T(8,128)}, u32[]{:S(2)}, u32[]{:S(2)}) %collective-permute-start.5) | collective-permute-done | bytes 262176 | tf_op jit(solution)/shard_map/ppermute | solution.py:84
  223.2 2.8 convolution_bitcast_fusion.2
  229.0 14.6 %all_gather.26 = f32[1024,128]{0,1:T(8,128)S(1)} all-gather(f32[128,128]{0,1:T(8,128)S(1)} %add_add_fusion.1), channel_id=1, replica_groups=mesh['grp'=4,'sub'=8] {'sub'}, dimensions={0}, use_global_device_ids=true | all-gather | bytes 589824 | tf_op jit(solution)/shard_map/all_gather | solution.py:72
  244.5 2.1 copy.95
  246.6 2.1 convolution_multiply_fusion
  249.9 2.5 copy.97
  252.5 7.2 %fusion.33 = f32[2,1024,128]{1,2,0:T(8,128)S(1)} fusion(f32[2,1024,128]{1,2,0:T(8,128)} %copy.97, f32[128,512,1]{1,0,2:T(8,128)} %convolution_bitcast_fusion.2, f32[1,2,1024,512]{3,2,1,0:T(8,128)} %param.15, f32[1,2,1024,128]{2,3,1,0:T(8,128)} %copy-done.2, f32[2,1024]{1,0:T(2,128)S(1)} %compare_convert_fusion), kind=kOutput, calls=%fused_computation.23 | convolution fusion | flops 1611399168 | bytes 7610368 | tf_op jit(solution)/shard_map/jrs,sl->jrl/dot_general | solution.py:77
  259.7 12.1 %fusion.66 = f32[2,128,1024]{2,1,0:T(8,128)} fusion(f32[2,1024,128]{1,2,0:T(8,128)S(1)} %fusion.33, f32[1,2,1024,1024]{3,2,1,0:T(8,128)} %param.14, f32[2,1024]{1,0:T(2,128)S(1)} %compare_convert_fusion), kind=kOutput, calls=%fused_computation.37 | convolution fusion | flops 3221487616 | bytes 10493952 | tf_op jit(solution)/shard_map/jrc,jcl->jrl/dot_general | solution.py:79
  271.8 2.6 copy.99
  274.4 2.4 reshape.169
  276.8 2.4 fusion.81
  280.4 4.2 %all-to-all-start.2 = ((f32[8,2,128,128]{3,2,1,0:T(8,128)}), f32[8,2,128,128]{3,2,1,0:T(8,128)}, u32[]{:S(2)}, u32[]{:S(2)}) async-start(f32[8,2,128,128]{3,2,1,0:T(8,128)} %copy.101), calls=%async_computation.5 | async-start | bytes 2097152 | tf_op jit(solution)/shard_map/all_to_all | solution.py:96
  284.9 5.3 %fusion.75 = f32[512,128]{0,1:T(8,128)} fusion(f32[1,2,1024,512]{3,2,1,0:T(8,128)} %param.15, f32[2,128,1024]{2,1,0:T(8,128)S(1)} %copy-done.1), kind=kOutput, calls=%fused_computation.42 | convolution fusion | flops 1610612736 | bytes 5505024 | tf_op jit(solution)/shard_map/jrs,jrl->sl/dot_general | solution.py:80
  290.6 10.7 %all_gather.27 = f32[512,128]{0,1:T(8,128)S(1)} all-gather(f32[128,128]{0,1:T(8,128)S(1)} %add_add_fusion.1), channel_id=1, replica_groups=mesh['grp'=4,'sub'=8] {'grp'}, dimensions={0}, use_global_device_ids=true | all-gather | bytes 327680 | tf_op jit(solution)/shard_map/all_gather | solution.py:61
  301.2 3.1 convolution_bitcast_fusion
  305.4 2.0 collective-permute-start.7
  307.5 10.5 %collective-permute-done.7 = f32[512,128]{0,1:T(8,128)S(1)} collective-permute-done((f32[512,128]{0,1:T(8,128)S(1)}, f32[512,128]{0,1:T(8,128)S(1)}, u32[]{:S(2)}, u32[]{:S(2)}) %collective-permute-start.7) | collective-permute-done | bytes 262176 | tf_op jit(solution)/shard_map/ppermute | solution.py:84
  320.0 15.3 %collective-permute-done.8 = f32[512,128]{0,1:T(8,128)} collective-permute-done((f32[512,128]{0,1:T(8,128)}, f32[512,128]{0,1:T(8,128)}, u32[]{:S(2)}, u32[]{:S(2)}) %collective-permute-start.8) | collective-permute-done | bytes 262176 | tf_op jit(solution)/shard_map/ppermute | solution.py:84
  335.3 3.2 fusion.87
  (90 shorter events, 34.3 us)
Async XLA Ops:
  7.2 11.0 %copy-start = (f32[1024,512]{1,0:T(8,128)S(1)}, f32[1024,512]{1,0:T(8,128)}, u32[]{:S(2)}) copy-start(f32[1024,512]{1,0:T(8,128)} %param.13) | copy-start | bytes 6291460
  7.2 29.7 %copy-start.10 = (s32[1,2,8,1]{2,3,1,0:T(1,128)S(1)}, s32[1,2,8,1]{2,3,1,0:T(1,128)}, u32[]{:S(2)}) copy-start(s32[1,2,8,1]{2,3,1,0:T(1,128)} %param.25) | copy-start | bytes 196
  7.2 30.4 %copy-start.12 = (s32[1,2]{1,0:T(1,128)S(1)}, s32[1,2]{1,0:T(1,128)}, u32[]{:S(2)}) copy-start(s32[1,2]{1,0:T(1,128)} %param.24) | copy-start | bytes 28
  7.2 30.6 %copy-start.5 = (f32[1,2,8,128]{3,2,1,0:T(8,128)S(1)}, f32[1,2,8,128]{3,2,1,0:T(8,128)}, u32[]{:S(2)}) copy-start(f32[1,2,8,128]{3,2,1,0:T(8,128)} %param.21) | copy-start | bytes 24580
  7.2 107.0 %reduce-scatter.4.cloned.1.call-start = ((), (), s32[]{:S(2)}) async-start(), calls=%async_computation.6 | async-start | bytes 589824 | tf_op jit(solution)/shard_map/reduce_scatter | solution.py:66
  20.7 20.1 %copy-start.11 = (s32[1,2]{1,0:T(1,128)S(1)}, s32[1,2]{1,0:T(1,128)}, u32[]{:S(2)}) copy-start(s32[1,2]{1,0:T(1,128)} %param.23) | copy-start | bytes 28
  20.8 21.8 %copy-start.6 = (f32[1,2,8,128]{3,2,1,0:T(8,128)S(1)}, f32[1,2,8,128]{3,2,1,0:T(8,128)}, u32[]{:S(2)}) copy-start(f32[1,2,8,128]{3,2,1,0:T(8,128)} %param.22) | copy-start | bytes 24580
  37.6 12.2 %copy-start.9 = (s32[16]{0:T(128)}, s32[16]{0:T(128)S(1)}, u32[]{:S(2)}) copy-start(s32[16]{0:T(128)S(1)} %eq.58) | copy-start | bytes 196
  42.5 19.4 %copy-start.2 = (f32[1,2,1024,128]{2,3,1,0:T(8,128)}, f32[1,2,1024,128]{2,3,1,0:T(8,128)S(1)}, u32[]{:S(2)}) copy-start(f32[1,2,1024,128]{2,3,1,0:T(8,128)S(1)} %copy.77) | copy-start | bytes 3145732
  42.5 22.4 %copy-start.7 = (s32[16]{0:T(128)}, s32[16]{0:T(128)S(1)}, u32[]{:S(2)}) copy-start(s32[16]{0:T(128)S(1)} %multiply_add_fusion.1) | copy-start | bytes 196
  68.6 43.7 %all-to-all-start = ((f32[8,2,128,128]{3,2,1,0:T(8,128)}), f32[8,2,128,128]{3,2,1,0:T(8,128)}, u32[]{:S(2)}, u32[]{:S(2)}) async-start(f32[8,2,128,128]{3,2,1,0:T(8,128)} %copy.85), calls=%async_computation.1 | async-start | bytes 2097152 | tf_op jit(solution)/shard_map/all_to_all | solution.py:96
  73.9 65.7 %all-gather.3.cloned.1.call-start = ((), (), s32[]{:S(2)}) async-start(), calls=%async_computation.9 | async-start | bytes 1179648 | tf_op jit(solution)/shard_map/all_gather | solution.py:56
  79.7 1.7 collective-permute-start
  82.1 23.8 %collective-permute-start.1 = (f32[512,128]{0,1:T(8,128)}, f32[512,128]{0,1:T(8,128)}, u32[]{:S(2)}, u32[]{:S(2)}) collective-permute-start(f32[512,128]{0,1:T(8,128)} %add.67), channel_id=1, source_target_pairs={{0,2},{1,3},{2,0},{3,1},{4,6},{5,7},{6,4},{7,5},{8,10},{9,11},{10,... | collective-permute-start | bytes 786440 | tf_op jit(solution)/shard_map/ppermute | solution.py:84
  107.7 32.0 %collective-permute-start.2 = (f32[512,128]{0,1:T(8,128)}, f32[512,128]{0,1:T(8,128)}, u32[]{:S(2)}, u32[]{:S(2)}) collective-permute-start(f32[512,128]{0,1:T(8,128)} %add.68), channel_id=1, source_target_pairs={{0,4},{1,5},{2,6},{3,7},{4,0},{5,1},{6,2},{7,3},{8,12},{9,13},{10,... | collective-permute-start | bytes 786440 | tf_op jit(solution)/shard_map/ppermute | solution.py:84
  169.7 56.4 %all-to-all-start.1 = ((f32[8,2,128,128]{3,2,1,0:T(8,128)}), f32[8,2,128,128]{3,2,1,0:T(8,128)}, u32[]{:S(2)}, u32[]{:S(2)}) async-start(f32[8,2,128,128]{3,2,1,0:T(8,128)} %copy.92), calls=%async_computation.3 | async-start | bytes 2097152 | tf_op jit(solution)/shard_map/all_to_all | solution.py:96
  173.9 54.1 %reduce-scatter.6.cloned.1.call-start = ((), (), s32[]{:S(2)}) async-start(), calls=%async_computation.7 | async-start | bytes 589824 | tf_op jit(solution)/shard_map/reduce_scatter | solution.py:66
  185.4 23.2 %copy-start.4 = (f32[128,128]{1,0:T(8,128)S(1)}, f32[128,128]{1,0:T(8,128)}, u32[]{:S(2)}) copy-start(f32[128,128]{1,0:T(8,128)} %param.19) | copy-start | bytes 196612
  190.4 1.6 collective-permute-start.3
  192.0 15.0 %collective-permute-start.4 = (f32[512,128]{0,1:T(8,128)S(1)}, f32[512,128]{0,1:T(8,128)S(1)}, u32[]{:S(2)}, u32[]{:S(2)}) collective-permute-start(f32[512,128]{0,1:T(8,128)S(1)} %add.73), channel_id=1, source_target_pairs={{0,2},{1,3},{2,0},{3,1},{4,6},{5,7},{6,4},{7,5},{8,10},{9,11},{10,... | collective-permute-start | bytes 786440 | tf_op jit(solution)/shard_map/ppermute | solution.py:84
  207.8 15.4 %collective-permute-start.5 = (f32[512,128]{0,1:T(8,128)}, f32[512,128]{0,1:T(8,128)}, u32[]{:S(2)}, u32[]{:S(2)}) collective-permute-start(f32[512,128]{0,1:T(8,128)} %add.74), channel_id=1, source_target_pairs={{0,4},{1,5},{2,6},{3,7},{4,0},{5,1},{6,2},{7,3},{8,12},{9,13},{10,... | collective-permute-start | bytes 786440 | tf_op jit(solution)/shard_map/ppermute | solution.py:84
  271.8 4.9 %copy-start.8 = (s32[16]{0:T(128)S(1)}, s32[16]{0:T(128)}, u32[]{:S(2)}) copy-start(s32[16]{0:T(128)} %copy-done.7) | copy-start | bytes 196
  279.2 5.7 %copy-start.1 = (f32[2,128,1024]{2,1,0:T(8,128)S(1)}, f32[2,128,1024]{2,1,0:T(8,128)}, u32[]{:S(2)}) copy-start(f32[2,128,1024]{2,1,0:T(8,128)} %fusion.66) | copy-start | bytes 3145732
  280.4 58.8 %all-to-all-start.2 = ((f32[8,2,128,128]{3,2,1,0:T(8,128)}), f32[8,2,128,128]{3,2,1,0:T(8,128)}, u32[]{:S(2)}, u32[]{:S(2)}) async-start(f32[8,2,128,128]{3,2,1,0:T(8,128)} %copy.101), calls=%async_computation.5 | async-start | bytes 2097152 | tf_op jit(solution)/shard_map/all_to_all | solution.py:96
  284.6 55.9 %reduce-scatter.8.cloned.1.call-start = ((), (), s32[]{:S(2)}) async-start(), calls=%async_computation.8 | async-start | bytes 589824 | tf_op jit(solution)/shard_map/reduce_scatter | solution.py:66
  290.2 14.1 %collective-permute-start.6 = (f32[512,128]{0,1:T(8,128)}, f32[512,128]{0,1:T(8,128)}, u32[]{:S(2)}, u32[]{:S(2)}) collective-permute-start(f32[512,128]{0,1:T(8,128)} %fusion.75), channel_id=1, source_target_pairs={{0,1},{1,0},{2,3},{3,2},{4,5},{5,4},{6,7},{7,6},{8,9},{9,8},{10,11... | collective-permute-start | bytes 786440 | tf_op jit(solution)/shard_map/ppermute | solution.py:84
  304.3 36.3 %copy-start.3 = (f32[128,128]{0,1:T(8,128)S(1)}, f32[128,128]{0,1:T(8,128)}, u32[]{:S(2)}) copy-start(f32[128,128]{0,1:T(8,128)} %copy.89) | copy-start | bytes 196612
  305.4 12.6 %collective-permute-start.7 = (f32[512,128]{0,1:T(8,128)S(1)}, f32[512,128]{0,1:T(8,128)S(1)}, u32[]{:S(2)}, u32[]{:S(2)}) collective-permute-start(f32[512,128]{0,1:T(8,128)S(1)} %add.78), channel_id=1, source_target_pairs={{0,2},{1,3},{2,0},{3,1},{4,6},{5,7},{6,4},{7,5},{8,10},{9,11},{10,... | collective-permute-start | bytes 786440 | tf_op jit(solution)/shard_map/ppermute | solution.py:84
  318.7 16.6 %collective-permute-start.8 = (f32[512,128]{0,1:T(8,128)}, f32[512,128]{0,1:T(8,128)}, u32[]{:S(2)}, u32[]{:S(2)}) collective-permute-start(f32[512,128]{0,1:T(8,128)} %add.79), channel_id=1, source_target_pairs={{0,4},{1,5},{2,6},{3,7},{4,0},{5,1},{6,2},{7,3},{8,12},{9,13},{10,... | collective-permute-start | bytes 786440 | tf_op jit(solution)/shard_map/ppermute | solution.py:84
Sparse Core Ops, SparseCore 0:
  20.9 31.6 reduce-scatter.3
  76.4 32.4 all-gather.2
  185.5 32.6 reduce-scatter.5
  304.5 32.2 reduce-scatter.7
